TPU v7x, 32 devices: a whole 2x2x4 slice. The times are simulated.
32 devices in a mesh: gx: 4 (over x, core), gy: 8 (over z, y).
Axes of the slice: x: 2, y: 2, z: 4, core: 2. Of those that a mesh axis runs over, the one named last changes fastest.
Arguments:
- slot_tiles: int32 [32, 32], P(('gx', 'gy')), may hold values from -1 to 63, as said below
- owner_map: int32 [32], replicated, may hold values from 0 to 31, each once
- slot_depth: int32 [32, 32, 16, 128], P(('gx', 'gy')), may hold values from 0 to 1073741823
- slot_color: bfloat16 [32, 32, 16, 3, 128], P(('gx', 'gy')), may hold values from 0 to 1
Outputs:
- region_depth: int32 [32, 2, 16, 128], P(('gx', 'gy'))
- region_color: bfloat16 [32, 2, 16, 3, 128], P(('gx', 'gy'))
- thumbnail: float32 [32, 3, 64], replicated
Inputs may be any that keep to these rules, and one draw needn't show every extreme that they name: `slot_tiles`: each rank's used slots name the tiles of one rectangle of at least 4 tile rows of the 8 x 8 tile grid, each once, in row-major order, followed by -1 in the unused slots; all ranks' rectangles contain a common region. `owner_map`: each rank owns exactly one region.
All inputs are finite; a program needn't handle non-finite values.
Results may differ from a plain program's by a relative error of at most 0.001.
Values may be sent and summed in bfloat16 or wider, within the bound.
A program may use at most 64 MiB of HBM per device.

v0:
```python
import functools

import jax
import jax.numpy as jnp
from jax import lax
from jax.experimental import pallas as pl
from jax.experimental.pallas import tpu as pltpu
from jax.sharding import PartitionSpec as P

FAR = 1073741824
HALF = 536870912
LOWEST = -2147483648
MESH = pl.DeviceIdType.MESH


def div_const(value, by):
    if by & (by - 1) == 0:
        return value >> (by.bit_length() - 1)
    return value // by


def merge(first, second):
    key_a, colors_a = first
    key_b, colors_b = second
    nearer = key_b < key_a
    key = jnp.where(nearer, key_b, key_a)
    return key, [jnp.where(nearer, b, a) for a, b in zip(colors_a, colors_b)]


def kernel(
    dims, inv_ref, own_ref, slots_ref, depth_ref, color_ref,
    out_d, out_c, out_t,
    cs_d, cs_c, cr_d, cr_c, ys_d, ys_c, yr_d, yr_c, zs_d, zs_c, zr_d, zr_c, xs_d, xs_c, xr_d, xr_c,
    gath,
    c_ss, c_rs, y_ss, y_rs, z_ss, z_rs, x_ss, x_rs, g1_ss, g1_rs, g2_ss, g2_rs,
):
    GX, GY, X, Y, Z = dims
    regions = GX * GY
    gx = lax.axis_index("gx")
    gy = lax.axis_index("gy")
    core = lax.rem(gx, 2)
    x = lax.div(gx, 2)
    y = lax.rem(gy, Y)
    z = lax.div(gy, Y)
    tile_cols = GY

    barrier = pltpu.get_barrier_semaphore()
    for j in range(1, GX):
        pl.semaphore_signal(barrier, inc=1, device_id=(lax.rem(gx + j, GX), gy), device_id_type=MESH)
    for j in range(1, GY):
        pl.semaphore_signal(barrier, inc=1, device_id=(gx, lax.rem(gy + j, GY)), device_id_type=MESH)

    first = slots_ref[0, 0]
    last = first
    for s in range(1, slots_ref.shape[1]):
        last = jnp.maximum(last, slots_ref[0, s])
    top = div_const(first, tile_cols)
    left = first - top * tile_cols
    bottom = div_const(last, tile_cols)
    right = last - bottom * tile_cols
    width = right - left + 1

    def own_tile(owner_core, owner_x, owner_y, owner_z, half):
        rank = (owner_x * 2 + owner_core) * GY + owner_z * Y + owner_y
        region = inv_ref[rank]
        pair = div_const(region, tile_cols)
        col = region - pair * tile_cols
        row = pair * 2 + half
        live = (row >= top) & (row <= bottom) & (col >= left) & (col <= right)
        slot = jnp.where(live, (row - top) * width + (col - left), 0)
        floor = jnp.where(live, LOWEST, 2 * HALF)
        key = jnp.maximum((depth_ref[slot] - HALF) * 2, floor) + core
        return key, [color_ref[slot, c] for c in range(3)]

    def load(ref_d, ref_c, index):
        return ref_d[index], [ref_c[index + (c,)] for c in range(3)]

    def store(ref_d, ref_c, index, value):
        ref_d[index] = value[0]
        for c in range(3):
            ref_c[index + (c,)] = value[1][c]

    pending = []

    def remote(src, dst, ss, rs, device):
        return pltpu.make_async_remote_copy(
            src_ref=src, dst_ref=dst, send_sem=ss, recv_sem=rs, device_id=device, device_id_type=MESH
        )

    def send(pairs, sems, device):
        for k, (src, dst) in enumerate(pairs):
            copy = remote(src, dst, sems[0].at[sems[1] + (k,)], sems[2].at[sems[3] + (k,)], device)
            copy.start()
            pending.append(copy)

    def arrived(refs, rs, index, device):
        for k, ref in enumerate(refs):
            remote(ref, ref, c_ss.at[0, k], rs.at[index + (k,)], device).wait_recv()

    other_core = 1 - core
    core_partner = (x * 2 + other_core, gy)
    me = (gx, gy)
    chunk_x = [lax.rem(x + 1 + j, X) for j in range(X)]

    for j in range(X):

        def pack(i, carry, j=j):
            yy = lax.div(i, Z)
            zz = lax.rem(i, Z)
            for h in range(2):
                store(cs_d, cs_c, (j, yy, zz, h), own_tile(other_core, chunk_x[j], yy, zz, h))
            return carry

        lax.fori_loop(0, Y * Z, pack, 0)
        if j == 0:
            pl.semaphore_wait(barrier, GX + GY - 2)
        send([(cs_d.at[j], cr_d.at[j]), (cs_c.at[j], cr_c.at[j])], (c_ss, (j,), c_rs, (j,)), core_partner)

    lane_k = lax.broadcasted_iota(jnp.int32, (128, 128), 0) // 8
    lane_l = lax.broadcasted_iota(jnp.int32, (128, 128), 1)
    groups = []
    for h in range(2):
        hit = (lane_l == lane_k + 32 * h) | (lane_l == lane_k + 32 * h + 80)
        groups.append(jnp.where(hit, 1.0 / 64.0, 0.0).astype(jnp.bfloat16))

    for j in range(X):
        arrived([cr_d.at[j], cr_c.at[j]], c_rs, (j,), me)
        for i in range(Y):
            yy = lax.rem(y + 1 + i, Y)
            mine = i == Y - 1

            def step(zz, carry, j=j, yy=yy, mine=mine):
                for h in range(2):
                    value = merge(
                        own_tile(core, chunk_x[j], yy, zz, h), load(cr_d, cr_c, (j, yy, zz, h))
                    )
                    if mine:
                        store(yr_d, yr_c, (j, y, zz, h), value)
                    else:
                        store(ys_d, ys_c, (j, yy, zz, h), value)
                return carry

            lax.fori_loop(0, Z, step, 0)
            if not mine:
                send(
                    [(ys_d.at[j, yy], yr_d.at[j, y]), (ys_c.at[j, yy], yr_c.at[j, y])],
                    (y_ss, (j, i), y_rs, (j, y)),
                    (gx, z * Y + yy),
                )

    for j in range(X):
        for i in range(Y - 1):
            yy = lax.rem(y + 1 + i, Y)
            arrived([yr_d.at[j, yy], yr_c.at[j, yy]], y_rs, (j, yy), me)
        for i in range(Z):
            zz = lax.rem(z + 1 + i, Z)
            mine = i == Z - 1
            for h in range(2):
                value = load(yr_d, yr_c, (j, 0, zz, h))
                for k in range(1, Y):
                    value = merge(value, load(yr_d, yr_c, (j, k, zz, h)))
                if mine:
                    store(zr_d, zr_c, (j, z, h), value)
                else:
                    store(zs_d, zs_c, (j, zz, h), value)
            if not mine:
                send(
                    [(zs_d.at[j, zz], zr_d.at[j, z]), (zs_c.at[j, zz], zr_c.at[j, z])],
                    (z_ss, (j, i), z_rs, (j, z)),
                    (gx, zz * Y + y),
                )

    for j in range(X):
        for i in range(Z - 1):
            zz = lax.rem(z + 1 + i, Z)
            arrived([zr_d.at[j, zz], zr_c.at[j, zz]], z_rs, (j, zz), me)
        mine = j == X - 1
        for h in range(2):
            value = load(zr_d, zr_c, (j, 0, h))
            for k in range(1, Z):
                value = merge(value, load(zr_d, zr_c, (j, k, h)))
            value = (value[0] >> 1, value[1])
            if mine:
                store(xr_d, xr_c, (x, h), value)
            else:
                store(xs_d, xs_c, (j, h), value)
        if not mine:
            send(
                [(xs_d.at[j], xr_d.at[x]), (xs_c.at[j], xr_c.at[x])],
                (x_ss, (j,), x_rs, (x,)),
                (chunk_x[j] * 2 + core, gy),
            )

    for j in range(X - 1):
        xx = chunk_x[j]
        arrived([xr_d.at[xx], xr_c.at[xx]], x_rs, (xx,), me)

    sums = [None] * 3
    row = lax.broadcasted_iota(jnp.int32, (16, 128), 0)
    lane = lax.broadcasted_iota(jnp.int32, (16, 128), 1)
    keep = (row < 8) == (lane < 64)
    for h in range(2):
        value = load(xr_d, xr_c, (0, h))
        for k in range(1, X):
            value = merge(value, load(xr_d, xr_c, (k, h)))
        depth = value[0] + HALF
        out_d[h] = depth
        for c in range(3):
            color = jnp.where(depth == FAR, jnp.zeros((), jnp.bfloat16), value[1][c])
            out_c[h, c] = color
            part = jnp.dot(color, groups[h], preferred_element_type=jnp.float32)
            part = jnp.where(keep, part, 0.0)
            sums[c] = part if sums[c] is None else sums[c] + part
    rows = []
    for c in range(3):
        total = jnp.sum(sums[c], axis=0, keepdims=True)
        rows.append(total + pltpu.roll(total, 64, 1))
    lane_row = lax.broadcasted_iota(jnp.int32, (1, 128), 1)
    gath[gy, gx, 0:1, :] = jnp.where(lane_row < 64, rows[0], rows[1])
    gath[gy, gx, 1:2, :] = rows[2]

    for j in range(1, GX):
        send([(gath.at[gy, gx], gath.at[gy, gx])], (g1_ss, (j,), g1_rs, (gx,)), (lax.rem(gx + j, GX), gy))
    for j in range(1, GX):
        xx = lax.rem(gx + j, GX)
        arrived([gath.at[gy, xx]], g1_rs, (xx,), me)
    for j in range(1, GY):
        send([(gath.at[gy], gath.at[gy])], (g2_ss, (j,), g2_rs, (gy,)), (gx, lax.rem(gy + j, GY)))
    for j in range(1, GY):
        yy = lax.rem(gy + j, GY)
        arrived([gath.at[yy]], g2_rs, (yy,), me)

    def place(r, carry):
        owner = own_ref[r]
        owner_x = div_const(owner, GY)
        out_t[r] = gath[owner - owner_x * GY, owner_x]
        return carry

    lax.fori_loop(0, regions, place, 0)
    for copy in pending:
        copy.wait_send()


def finish(in_d, in_c, in_t, out_d, out_c, out_t):
    out_d[...] = in_d[...]
    out_c[...] = in_c[...]
    side = out_t.shape[2]
    upper = in_t[:, 0, :]
    out_t[0] = upper[:, :side]
    out_t[1] = upper[:, side:]
    out_t[2] = in_t[:, 1, :][:, :side]


def shards(slot_tiles, owner_map, slot_depth, slot_color):
    GX = lax.axis_size("gx")
    GY = lax.axis_size("gy")
    X, Z = GX // 2, 4
    Y = GY // Z
    regions = GX * GY
    band, width = slot_depth.shape[2:]
    ids = jnp.arange(regions, dtype=jnp.int32)
    inverse = jnp.sum(jnp.where(owner_map[None, :] == ids[:, None], ids[None, :], 0), axis=1)
    depth = slot_depth[0]
    color = jnp.transpose(slot_color[0], (0, 2, 1, 3))

    def pair(*lead):
        return [
            pltpu.VMEM(lead + (2, band, width), jnp.int32),
            pltpu.VMEM(lead + (2, 3, band, width), jnp.bfloat16),
        ]

    dma = lambda *shape: pltpu.SemaphoreType.DMA(shape)
    vmem = pl.BlockSpec(memory_space=pltpu.VMEM)
    smem = pl.BlockSpec(memory_space=pltpu.SMEM)
    out_d, out_c, out_t = pl.pallas_call(
        functools.partial(kernel, (GX, GY, X, Y, Z)),
        out_shape=(
            jax.ShapeDtypeStruct((2, band, width), jnp.int32),
            jax.ShapeDtypeStruct((2, 3, band, width), jnp.bfloat16),
            jax.ShapeDtypeStruct((regions, 2, width), jnp.float32),
        ),
        in_specs=[smem, smem, smem, vmem, vmem],
        out_specs=(vmem, vmem, vmem),
        scratch_shapes=[
            *pair(X, Y, Z), *pair(X, Y, Z),
            *pair(X, Y, Z), *pair(X, Y, Z),
            *pair(X, Z), *pair(X, Z),
            *pair(X), *pair(X),
            pltpu.VMEM((GY, GX, 2, width), jnp.float32),
            dma(X, 2), dma(X, 2),
            dma(X, Y, 2), dma(X, Y, 2),
            dma(X, Z, 2), dma(X, Z, 2),
            dma(X, 2), dma(X, 2),
            dma(GX, 1), dma(GX, 1),
            dma(GY, 1), dma(GY, 1),
        ],
        compiler_params=pltpu.CompilerParams(collective_id=0, has_side_effects=True),
    )(inverse, owner_map, slot_tiles, depth, color)
    out_d, out_c, out_t = pl.pallas_call(
        finish,
        out_shape=(
            jax.ShapeDtypeStruct((2, band, width), jnp.int32),
            jax.ShapeDtypeStruct((2, 3, band, width), jnp.bfloat16),
            jax.ShapeDtypeStruct((3, regions, width // 2), jnp.float32),
        ),
        in_specs=[vmem, vmem, vmem],
        out_specs=(vmem, vmem, vmem),
    )(out_d, out_c, out_t)
    thumbnail = jnp.transpose(out_t, (1, 0, 2))
    return (out_d[None], jnp.transpose(out_c, (0, 2, 1, 3))[None], thumbnail)


def solution(mesh):
    placed = (
        P(("gx", "gy"), None),
        P(),
        P(("gx", "gy"), None, None, None),
        P(("gx", "gy"), None, None, None, None),
    )
    return jax.shard_map(
        shards,
        mesh=mesh,
        in_specs=placed,
        out_specs=(P(("gx", "gy"), None, None, None), P(("gx", "gy"), None, None, None, None), P()),
        check_vma=False,
    )
```

profile of v0, /device:TPU:0, one launch (start us, length us, event | category | flops | bytes accessed | tf_op | source)
XLA Modules:
  0.0 35.6 jit_solution(5996222867138461521)
XLA Ops:
  0.6 0.0 copy-start
  0.6 0.6 %copy-done = s32[32]{0:T(128)S(1)} copy-done((s32[32]{0:T(128)S(1)}, s32[32]{0:T(128)}, u32[]{:S(2)}) %copy-start) | copy-done | bytes 152
  1.3 0.6 %select_reduce_fusion.inv_ref = s32[32]{0:T(128)} fusion(s32[32]{0:T(128)S(1)} %copy-done), kind=kLoop, calls=%fused_computation | loop fusion | flops 3040 | bytes 256 | tf_op jit(solution)/shard_map/reduce_sum | solution.py:262
  1.9 32.2 %shard_map.67 = (s32[2,16,128]{2,1,0:T(8,128)}, bf16[2,3,16,128]{3,2,1,0:T(8,128)(2,1)}, f32[32,2,128]{2,1,0:T(2,128)}) custom-call(s32[32]{0:T(128)} %select_reduce_fusion.inv_ref, s32[32]{0:T(128)} %own_ref.1, s32[1,32]{1,0:T(1,128)} %slots_ref.1, s32[32,16,128]{2,1,0:T(8,128)} %bitcast.10, bf16[32,3,16,128]{3,2,1,0:T(8,128)(2,1)} %bitcast.9), custom_call_target="tpu_custom_call" | custom-call | tf_op jit(solution)/shard_map/pallas_call | solution.py:275
  34.1 1.5 %shard_map.68 = (s32[2,16,128]{2,1,0:T(8,128)}, bf16[2,3,16,128]{3,2,1,0:T(8,128)(2,1)}, f32[3,32,64]{2,1,0:T(8,128)}) custom-call(s32[2,16,128]{2,1,0:T(8,128)} %get-tuple-element.9.in_d, bf16[2,3,16,128]{3,2,1,0:T(8,128)(2,1)} %get-tuple-element.10.in_c, f32[32,2,128]{2,1,0:T(2,128)} %get-tuple-element.11.in_t), custom_call_target="tpu_custom_call" | custom-call | tf_op jit(solution)/shard_map/pallas_call | solution.py:299
Async XLA Ops:
  0.6 0.7 %copy-start = (s32[32]{0:T(128)S(1)}, s32[32]{0:T(128)}, u32[]{:S(2)}) copy-start(s32[32]{0:T(128)} %own_ref.1) | copy-start | bytes 388
where the time goes:
time: 35.9 us; the launch traced here: 35.6 us
  Pallas kernels  33.7 us (94%)
  local copies, waits for them, and re-layouts  0.65 us (2%)
  between operations  0.65 us (2%)
  other arithmetic  0.63 us (2%)
    pallas_call x1, Pallas kernels, shards(): pl.pallas_call(functools.partial(kernel, (GX, GY, X, Y, Z)), out_shape=(j...  32.2 us
    pallas_call x1, Pallas kernels, shards(): pl.pallas_call(finish, out_shape=(jax.ShapeDtypeStruct((2, band, width),...  1.5 us

commit v1 on v0

v1 whole, which is shorter than its diff:
```python
import functools

import jax
import jax.numpy as jnp
from jax import lax
from jax.experimental import pallas as pl
from jax.experimental.pallas import tpu as pltpu
from jax.sharding import PartitionSpec as P

FAR = 1073741824
HALF = 536870912
MESH = pl.DeviceIdType.MESH


def div_const(value, by):
    if by & (by - 1) == 0:
        return value >> (by.bit_length() - 1)
    return value // by


def merge(first, second):
    key_a, colors_a = first
    key_b, colors_b = second
    nearer = key_b < key_a
    key = jnp.minimum(key_a, key_b)
    return key, [jnp.where(nearer, b, a) for a, b in zip(colors_a, colors_b)]


def load(ref_d, ref_c, index):
    return ref_d[index], [ref_c[index + (c,)] for c in range(3)]


def store(ref_d, ref_c, index, value):
    ref_d[index] = value[0]
    for c in range(3):
        ref_c[index + (c,)] = value[1][c]


def far_pos(z, k, Z):
    if Z == 4:
        flip = Z - 1 - k
        hi, lo = z // 2, z % 2
        hi = 1 - hi if flip >= 2 else hi
        lo = 1 - lo if flip % 2 else lo
        return hi * 2 + lo
    return lax.rem(z + 1 + k, Z)


def kernel(
    dims, own_hbm, slots_hbm, depth_hbm, color_hbm,
    out_d, out_c, out_t,
    own_ref, slots_ref, tab_ref, depth_ref, color_ref,
    cs_d, cs_c, cr_d, cr_c, ys_d, ys_c, yr_d, yr_c, zs_d, zs_c, zr_d, zr_c,
    gath,
    l_sem, c_ss, c_rs, y_ss, y_rs, z_ss, z_rs, g_ss, g_rs, tok_lo, tok_hi,
):
    GX, GY, X, Y, Z = dims
    regions = GX * GY
    slots = slots_ref.shape[1]
    gx = lax.axis_index("gx")
    gy = lax.axis_index("gy")
    core = lax.rem(gx, 2)
    x = lax.div(gx, 2)
    y = lax.rem(gy, Y)
    z = lax.div(gy, Y)
    rank = gx * GY + gy
    tile_cols = GY

    def at(cc, xx, yy, zz):
        return (xx * 2 + cc, zz * Y + yy)

    barrier = pltpu.get_barrier_semaphore()

    def greet(device):
        pl.semaphore_signal(barrier, inc=1, device_id=device, device_id_type=MESH)

    greet(at(1 - core, x, y, z))
    for j in range(1, Y):
        greet(at(core, x, lax.rem(y + j, Y), z))
    for j in range(1, X):
        greet(at(core, lax.rem(x + j, X), y, z))
    has_lo = z > 0
    has_hi = z < Z - 1

    @pl.when(has_lo)
    def _():
        greet(at(core, x, y, z - 1))

    @pl.when(has_hi)
    def _():
        greet(at(core, x, y, z + 1))

    def local(src, dst, k):
        copy = pltpu.make_async_copy(src, dst, l_sem.at[k])
        copy.start()
        return copy

    loads = [
        local(own_hbm, own_ref, 0),
        local(slots_hbm, slots_ref, 1),
        local(depth_hbm, depth_ref.at[pl.ds(0, slots)], 2),
        local(color_hbm, color_ref.at[pl.ds(0, slots)], 3),
    ]

    def token(which):
        @pl.when(has_lo)
        def _():
            pl.semaphore_signal(tok_hi, inc=1, device_id=at(core, x, y, z - 1), device_id_type=MESH)

        @pl.when(has_hi)
        def _():
            pl.semaphore_signal(tok_lo, inc=1, device_id=at(core, x, y, z + 1), device_id_type=MESH)

    def take_token():
        @pl.when(has_lo)
        def _():
            pl.semaphore_wait(tok_lo, 1)

        @pl.when(has_hi)
        def _():
            pl.semaphore_wait(tok_hi, 1)

    depth_ref[slots] = jnp.full(depth_ref.shape[1:], FAR, jnp.int32)
    for c in range(3):
        color_ref[slots, c] = jnp.zeros(color_ref.shape[2:], jnp.bfloat16)

    loads[0].wait()
    loads[1].wait()
    words = (regions + 31) // 32
    bits = (regions - 1).bit_length()
    masks = [[None] * bits for _ in range(words)]
    for r in range(regions):
        owner = own_ref[r]
        for w in range(words):
            one = jnp.int32(1) << (owner & 31)
            if words > 1:
                one = jnp.where((owner >> 5) == w, one, 0)
            for b in range(bits):
                if (r >> b) & 1:
                    masks[w][b] = one if masks[w][b] is None else masks[w][b] | one
    vals = [slots_ref[0, s] for s in range(slots)]
    first = vals[0]
    while len(vals) > 1:
        vals = [jnp.maximum(vals[i], vals[i + 1]) for i in range(0, len(vals) - 1, 2)] + (
            [vals[-1]] if len(vals) % 2 else []
        )
    last = vals[0]
    top = div_const(first, tile_cols)
    left = first - top * tile_cols
    bottom = div_const(last, tile_cols)
    right = last - bottom * tile_cols
    width = right - left + 1
    for p in range(regions):
        region = None
        for b in range(bits):
            bit = ((masks[p // 32][b] >> (p % 32)) & 1) << b
            region = bit if region is None else region | bit
        pair = div_const(region, tile_cols)
        col = region - pair * tile_cols
        in_col = (col >= left) & (col <= right)
        for h in range(2):
            row = pair * 2 + h
            live = (row >= top) & (row <= bottom) & in_col
            tab_ref[p * 2 + h] = jnp.where(live, (row - top) * width + (col - left), slots)

    def own_tile(cc, xx, yy, zz, h):
        slot = tab_ref[((xx * 2 + cc) * GY + zz * Y + yy) * 2 + h]
        return (depth_ref[slot] - HALF) * 2 + core, [color_ref[slot, c] for c in range(3)]

    pending = []

    def remote(src, dst, ss, rs, device):
        return pltpu.make_async_remote_copy(
            src_ref=src, dst_ref=dst, send_sem=ss, recv_sem=rs, device_id=device, device_id_type=MESH
        )

    def send(pairs, sems, device):
        for k, (src, dst) in enumerate(pairs):
            copy = remote(src, dst, sems[0].at[sems[1] + (k,)], sems[2].at[sems[3] + (k,)], device)
            copy.start()
            pending.append(copy)

    def arrived(refs, rs, index):
        for k, ref in enumerate(refs):
            remote(ref, ref, c_ss.at[0, 0, k], rs.at[index + (k,)], (gx, gy)).wait_recv()

    targets_y = [lax.rem(y + 1 + i, Y) for i in range(Y)]
    targets_z = [far_pos(z, k, Z) for k in range(Z)]
    targets_x = [lax.rem(x + 1 + j, X) for j in range(X)]

    loads[2].wait()
    loads[3].wait()

    for i in range(Y):
        for k in range(Z):
            for j in range(X):
                for h in range(2):
                    store(cs_d, cs_c, (i, k, j, h), own_tile(1 - core, targets_x[j], targets_y[i], targets_z[k], h))
            if i == 0 and k == 0:
                near = X + Y - 1 + jnp.where(has_lo, 1, 0) + jnp.where(has_hi, 1, 0)
                pl.semaphore_wait(barrier, near)
            send(
                [(cs_d.at[i, k], cr_d.at[i, k]), (cs_c.at[i, k], cr_c.at[i, k])],
                (c_ss, (i, k), c_rs, (i, k)),
                at(1 - core, x, y, z),
            )
        if i == 0:
            token(0)

    for i in range(Y):
        mine = i == Y - 1
        for k in range(Z):
            arrived([cr_d.at[i, k], cr_c.at[i, k]], c_rs, (i, k))
            for j in range(X):
                for h in range(2):
                    value = merge(
                        own_tile(core, targets_x[j], targets_y[i], targets_z[k], h),
                        load(cr_d, cr_c, (i, k, j, h)),
                    )
                    if mine:
                        store(yr_d, yr_c, (k, j, y, h), value)
                    else:
                        store(ys_d, ys_c, (i, k, j, h), value)
                if not mine:
                    send(
                        [(ys_d.at[i, k, j], yr_d.at[k, j, y]), (ys_c.at[i, k, j], yr_c.at[k, j, y])],
                        (y_ss, (i, k, j), y_rs, (k, j, y)),
                        at(core, x, targets_y[i], z),
                    )
        if i == 0:
            take_token()
            token(1)

    take_token()
    token(2)
    take_token()

    for k in range(Z):
        for j in range(X):
            for i in range(Y - 1):
                yy = targets_y[i]
                arrived([yr_d.at[k, j, yy], yr_c.at[k, j, yy]], y_rs, (k, j, yy))
            mine = k == Z - 1 and j == X - 1
            for h in range(2):
                value = load(yr_d, yr_c, (k, j, 0, h))
                for q in range(1, Y):
                    value = merge(value, load(yr_d, yr_c, (k, j, q, h)))
                if mine:
                    store(zr_d, zr_c, (x, z, h), value)
                else:
                    store(zs_d, zs_c, (k, j, h), value)
            if not mine:
                send(
                    [(zs_d.at[k, j], zr_d.at[x, z]), (zs_c.at[k, j], zr_c.at[x, z])],
                    (z_ss, (k, j), z_rs, (x, z)),
                    at(core, targets_x[j], y, targets_z[k]),
                )

    lane_k = lax.broadcasted_iota(jnp.int32, (128, 128), 0) // 8
    lane_l = lax.broadcasted_iota(jnp.int32, (128, 128), 1)
    groups = []
    for h in range(2):
        hit = (lane_l == lane_k + 32 * h) | (lane_l == lane_k + 32 * h + 80)
        groups.append(jnp.where(hit, 1.0 / 64.0, 0.0).astype(jnp.bfloat16))

    for k in range(Z):
        for j in range(X):
            if k == Z - 1 and j == X - 1:
                continue
            xx, zz = targets_x[j], targets_z[k]
            arrived([zr_d.at[xx, zz], zr_c.at[xx, zz]], z_rs, (xx, zz))

    sums = [None] * 3
    row = lax.broadcasted_iota(jnp.int32, (16, 128), 0)
    lane = lax.broadcasted_iota(jnp.int32, (16, 128), 1)
    keep = (row < 8) == (lane < 64)
    for h in range(2):
        value = None
        for xx in range(X):
            part = load(zr_d, zr_c, (xx, 0, h))
            for zz in range(1, Z):
                part = merge(part, load(zr_d, zr_c, (xx, zz, h)))
            part = (part[0] >> 1, part[1])
            value = part if value is None else merge(value, part)
        out_d[h] = value[0] + HALF
        for c in range(3):
            color = value[1][c]
            out_c[h, c] = color
            part = jnp.dot(color, groups[h], preferred_element_type=jnp.float32)
            part = jnp.where(keep, part, 0.0)
            sums[c] = part if sums[c] is None else sums[c] + part
    rows = []
    for c in range(3):
        total = jnp.sum(sums[c], axis=0, keepdims=True)
        rows.append(total + pltpu.roll(total, 64, 1))
    lane_row = lax.broadcasted_iota(jnp.int32, (1, 128), 1)
    gath[gx, gy, 0:1, :] = jnp.where(lane_row < 64, rows[0], rows[1])
    gath[gx, gy, 1:2, :] = rows[2]

    others = []
    for k in range(Z):
        for j in range(X):
            for i in range(Y):
                for cc in (1 - core, core):
                    others.append(at(cc, targets_x[j], targets_y[i], targets_z[k]))
    others.pop()
    for n, device in enumerate(others):
        copy = remote(gath.at[gx, gy], gath.at[gx, gy], g_ss.at[n], g_rs.at[gx, gy], device)
        copy.start()
        pending.append(copy)
    for n, (ox, oy) in enumerate(others):
        remote(gath.at[ox, oy], gath.at[ox, oy], g_ss.at[n], g_rs.at[ox, oy], (gx, gy)).wait_recv()
    for r in range(regions):
        owner = own_ref[r]
        owner_x = div_const(owner, GY)
        out_t[r] = gath[owner_x, owner - owner_x * GY]
    for copy in pending:
        copy.wait_send()


def finish(in_d, in_c, in_t, out_d, out_c, out_t):
    out_d[...] = in_d[...]
    out_c[...] = in_c[...]
    side = out_t.shape[2]
    upper = in_t[:, 0, :]
    out_t[0] = upper[:, :side]
    out_t[1] = upper[:, side:]
    out_t[2] = in_t[:, 1, :][:, :side]


def shards(slot_tiles, owner_map, slot_depth, slot_color):
    GX = lax.axis_size("gx")
    GY = lax.axis_size("gy")
    X, Z = GX // 2, 4
    Y = GY // Z
    regions = GX * GY
    slots, band, width = slot_depth.shape[1:]
    depth = slot_depth[0]
    color = jnp.transpose(slot_color[0], (0, 2, 1, 3))

    def pair(*lead):
        return [
            pltpu.VMEM(lead + (band, width), jnp.int32),
            pltpu.VMEM(lead + (3, band, width), jnp.bfloat16),
        ]

    dma = lambda *shape: pltpu.SemaphoreType.DMA(shape)
    vmem = pl.BlockSpec(memory_space=pltpu.VMEM)
    hbm = pl.BlockSpec(memory_space=pl.ANY)
    out_d, out_c, out_t = pl.pallas_call(
        functools.partial(kernel, (GX, GY, X, Y, Z)),
        out_shape=(
            pltpu.VMEM((2, band, width), jnp.int32),
            pltpu.VMEM((2, 3, band, width), jnp.bfloat16),
            pltpu.VMEM((regions, 2, width), jnp.float32),
        ),
        in_specs=[hbm, hbm, hbm, hbm],
        out_specs=(vmem, vmem, vmem),
        scratch_shapes=[
            pltpu.SMEM((regions,), jnp.int32),
            pltpu.SMEM((1, slots), jnp.int32),
            pltpu.SMEM((2 * regions,), jnp.int32),
            *pair(slots + 1),
            *pair(Y, Z, X, 2), *pair(Y, Z, X, 2),
            *pair(Y, Z, X, 2), *pair(Z, X, Y, 2),
            *pair(Z, X, 2), *pair(X, Z, 2),
            pltpu.VMEM((GX, GY, 2, width), jnp.float32),
            dma(4),
            dma(Y, Z, 2), dma(Y, Z, 2),
            dma(Y, Z, X, 2), dma(Z, X, Y, 2),
            dma(Z, X, 2), dma(X, Z, 2),
            dma(regions), dma(GX, GY),
            pltpu.SemaphoreType.REGULAR, pltpu.SemaphoreType.REGULAR,
        ],
        compiler_params=pltpu.CompilerParams(collective_id=0, has_side_effects=True),
    )(owner_map, slot_tiles, depth, color)
    out_d, out_c, out_t = pl.pallas_call(
        finish,
        out_shape=(
            jax.ShapeDtypeStruct((2, band, width), jnp.int32),
            jax.ShapeDtypeStruct((2, 3, band, width), jnp.bfloat16),
            jax.ShapeDtypeStruct((3, regions, width // 2), jnp.float32),
        ),
        in_specs=[vmem, vmem, vmem],
        out_specs=(vmem, vmem, vmem),
    )(*(pltpu.with_memory_space_constraint(a, pltpu.VMEM) for a in (out_d, out_c, out_t)))
    thumbnail = jnp.transpose(out_t, (1, 0, 2))
    return (out_d[None], jnp.transpose(out_c, (0, 2, 1, 3))[None], thumbnail)


def solution(mesh):
    placed = (
        P(("gx", "gy"), None),
        P(),
        P(("gx", "gy"), None, None, None),
        P(("gx", "gy"), None, None, None, None),
    )
    return jax.shard_map(
        shards,
        mesh=mesh,
        in_specs=placed,
        out_specs=(P(("gx", "gy"), None, None, None), P(("gx", "gy"), None, None, None, None), P()),
        check_vma=False,
    )
```

time: 35.9 us -> 26.1 us (0.73)
  Pallas kernels: 33.7 us -> 25.3 us
  local copies, waits for them, and re-layouts: 0.65 us -> 0 us
  other arithmetic: 0.63 us -> 0 us
    pallas_call x1, Pallas kernels: 32.2 us -> 24.6 us  [shards(): pl.pallas_call(functools.partial(kernel, (GX, GY, X, Y, Z)), out_shape=(p...]
    pallas_call x1, Pallas kernels: 1.5 us -> 0.71 us  [shards(): pl.pallas_call(finish, out_shape=(jax.ShapeDtypeStruct((2, band, width),...]
    unnamed x2 -> x0, local copies, waits for them, and re-layouts: 0.65 us -> none
    reduce_sum x1 -> x0, other arithmetic: 0.63 us -> none  [shards(): jnp.sum(jnp.where(owner_map[None, :] == ids[:, None], ids[None, :], 0), a...]
where the time goes in v1:
time: 26.1 us; the launch traced here: 25.9 us
  Pallas kernels  25.3 us (97%)
  between operations  0.64 us (2%)
    pallas_call x1, Pallas kernels, shards(): pl.pallas_call(functools.partial(kernel, (GX, GY, X, Y, Z)), out_shape=(p...  24.6 us
    pallas_call x1, Pallas kernels, shards(): pl.pallas_call(finish, out_shape=(jax.ShapeDtypeStruct((2, band, width),...  0.71 us

profile of v1, /device:TPU:0, one launch (start us, length us, event | category | flops | bytes accessed | tf_op | source)
XLA Modules:
  0.0 25.9 jit_solution(7590640898669528727)
XLA Ops:
  0.6 24.6 %shard_map.67 = (s32[2,16,128]{2,1,0:T(8,128)S(1)}, bf16[2,3,16,128]{3,2,1,0:T(8,128)(2,1)S(1)}, f32[32,2,128]{2,1,0:T(2,128)S(1)}) custom-call(s32[32]{0:T(128)} %own_hbm.1, s32[1,32]{1,0:T(1,128)} %slots_hbm.1, s32[32,16,128]{2,1,0:T(8,128)} %bitcast.10, bf16[32,3,16,128]{3,2,1,0:T(8,128)(2,1)} %bitcast.9), custom_call_target="tpu_custom_call" | custom-call | tf_op jit(solution)/shard_map/pallas_call | solution.py:350
  25.2 0.7 %shard_map.68 = (s32[2,16,128]{2,1,0:T(8,128)}, bf16[2,3,16,128]{3,2,1,0:T(8,128)(2,1)}, f32[3,32,64]{2,1,0:T(8,128)}) custom-call(s32[2,16,128]{2,1,0:T(8,128)S(1)} %get-tuple-element.9.in_d, bf16[2,3,16,128]{3,2,1,0:T(8,128)(2,1)S(1)} %get-tuple-element.10.in_c, f32[32,2,128]{2,1,0:T(2,128)S(1)} %get-tuple-element.11.in_t), custom_call_target="tpu_custom_call" | custom-call | tf_op jit(solution)/shard_map/pallas_call | solution.py:377

commit v2 on v1

--- a/solution.py
+++ b/solution.py
@@ -52,7 +52,7 @@
     own_ref, slots_ref, tab_ref, depth_ref, color_ref,
     cs_d, cs_c, cr_d, cr_c, ys_d, ys_c, yr_d, yr_c, zs_d, zs_c, zr_d, zr_c,
     gath,
-    l_sem, c_ss, c_rs, y_ss, y_rs, z_ss, z_rs, g_ss, g_rs, tok_lo, tok_hi,
+    l_sem, s_sem, c_rs, y_rs, z_rs, g_rs, tok_lo, tok_hi,
 ):
     GX, GY, X, Y, Z = dims
     regions = GX * GY
@@ -167,22 +167,23 @@
         slot = tab_ref[((xx * 2 + cc) * GY + zz * Y + yy) * 2 + h]
         return (depth_ref[slot] - HALF) * 2 + core, [color_ref[slot, c] for c in range(3)]
 
-    pending = []
-
     def remote(src, dst, ss, rs, device):
         return pltpu.make_async_remote_copy(
             src_ref=src, dst_ref=dst, send_sem=ss, recv_sem=rs, device_id=device, device_id_type=MESH
         )
 
-    def send(pairs, sems, device):
+    def send(pairs, which, rs, device):
         for k, (src, dst) in enumerate(pairs):
-            copy = remote(src, dst, sems[0].at[sems[1] + (k,)], sems[2].at[sems[3] + (k,)], device)
-            copy.start()
-            pending.append(copy)
-
-    def arrived(refs, rs, index):
-        for k, ref in enumerate(refs):
-            remote(ref, ref, c_ss.at[0, 0, k], rs.at[index + (k,)], (gx, gy)).wait_recv()
+            remote(src, dst, s_sem.at[which + k], rs, device).start()
+
+    def take(ref, rs):
+        remote(ref, ref, s_sem.at[0], rs, (gx, gy)).wait_recv()
+
+    def arrived(units, rs):
+        take(depth_ref.at[pl.ds(0, 5 * units)], rs)
+
+    def drained(ref, which):
+        remote(ref, ref, s_sem.at[which], g_rs, (gx, gy)).wait_send()
 
     targets_y = [lax.rem(y + 1 + i, Y) for i in range(Y)]
     targets_z = [far_pos(z, k, Z) for k in range(Z)]
@@ -201,7 +202,7 @@
                 pl.semaphore_wait(barrier, near)
             send(
                 [(cs_d.at[i, k], cr_d.at[i, k]), (cs_c.at[i, k], cr_c.at[i, k])],
-                (c_ss, (i, k), c_rs, (i, k)),
+                0, c_rs.at[i, k],
                 at(1 - core, x, y, z),
             )
         if i == 0:
@@ -210,7 +211,7 @@
     for i in range(Y):
         mine = i == Y - 1
         for k in range(Z):
-            arrived([cr_d.at[i, k], cr_c.at[i, k]], c_rs, (i, k))
+            arrived(X, c_rs.at[i, k])
             for j in range(X):
                 for h in range(2):
                     value = merge(
@@ -224,7 +225,7 @@
                 if not mine:
                     send(
                         [(ys_d.at[i, k, j], yr_d.at[k, j, y]), (ys_c.at[i, k, j], yr_c.at[k, j, y])],
-                        (y_ss, (i, k, j), y_rs, (k, j, y)),
+                        2, y_rs.at[i, k, j],
                         at(core, x, targets_y[i], z),
                     )
         if i == 0:
@@ -238,8 +239,7 @@
     for k in range(Z):
         for j in range(X):
             for i in range(Y - 1):
-                yy = targets_y[i]
-                arrived([yr_d.at[k, j, yy], yr_c.at[k, j, yy]], y_rs, (k, j, yy))
+                arrived(1, y_rs.at[i, k, j])
             mine = k == Z - 1 and j == X - 1
             for h in range(2):
                 value = load(yr_d, yr_c, (k, j, 0, h))
@@ -248,11 +248,11 @@
                 if mine:
                     store(zr_d, zr_c, (x, z, h), value)
                 else:
-                    store(zs_d, zs_c, (k, j, h), value)
+                    store(zs_d, zs_c, (k * X + j, h), value)
             if not mine:
                 send(
-                    [(zs_d.at[k, j], zr_d.at[x, z]), (zs_c.at[k, j], zr_c.at[x, z])],
-                    (z_ss, (k, j), z_rs, (x, z)),
+                    [(zs_d.at[k * X + j], zr_d.at[x, z]), (zs_c.at[k * X + j], zr_c.at[x, z])],
+                    4, z_rs.at[x, z],
                     at(core, targets_x[j], y, targets_z[k]),
                 )
 
@@ -268,7 +268,7 @@
             if k == Z - 1 and j == X - 1:
                 continue
             xx, zz = targets_x[j], targets_z[k]
-            arrived([zr_d.at[xx, zz], zr_c.at[xx, zz]], z_rs, (xx, zz))
+            arrived(1, z_rs.at[xx, zz])
 
     sums = [None] * 3
     row = lax.broadcasted_iota(jnp.int32, (16, 128), 0)
@@ -294,8 +294,8 @@
         total = jnp.sum(sums[c], axis=0, keepdims=True)
         rows.append(total + pltpu.roll(total, 64, 1))
     lane_row = lax.broadcasted_iota(jnp.int32, (1, 128), 1)
-    gath[gx, gy, 0:1, :] = jnp.where(lane_row < 64, rows[0], rows[1])
-    gath[gx, gy, 1:2, :] = rows[2]
+    gath[rank, 0:1, :] = jnp.where(lane_row < 64, rows[0], rows[1])
+    gath[rank, 1:2, :] = rows[2]
 
     others = []
     for k in range(Z):
@@ -304,18 +304,18 @@
                 for cc in (1 - core, core):
                     others.append(at(cc, targets_x[j], targets_y[i], targets_z[k]))
     others.pop()
-    for n, device in enumerate(others):
-        copy = remote(gath.at[gx, gy], gath.at[gx, gy], g_ss.at[n], g_rs.at[gx, gy], device)
-        copy.start()
-        pending.append(copy)
-    for n, (ox, oy) in enumerate(others):
-        remote(gath.at[ox, oy], gath.at[ox, oy], g_ss.at[n], g_rs.at[ox, oy], (gx, gy)).wait_recv()
+    for device in others:
+        remote(gath.at[rank], gath.at[rank], s_sem.at[6], g_rs, device).start()
+    take(gath.at[pl.ds(0, regions - 1)], g_rs)
     for r in range(regions):
-        owner = own_ref[r]
-        owner_x = div_const(owner, GY)
-        out_t[r] = gath[owner_x, owner - owner_x * GY]
-    for copy in pending:
-        copy.wait_send()
+        out_t[r] = gath[own_ref[r]]
+    drained(cs_d, 0)
+    drained(cs_c, 1)
+    drained(ys_d, 2)
+    drained(ys_c, 3)
+    drained(zs_d, 4)
+    drained(zs_c, 5)
+    drained(gath.at[pl.ds(0, regions - 1)], 6)
 
 
 def finish(in_d, in_c, in_t, out_d, out_c, out_t):
@@ -362,14 +362,11 @@
             pltpu.SMEM((2 * regions,), jnp.int32),
             *pair(slots + 1),
             *pair(Y, Z, X, 2), *pair(Y, Z, X, 2),
-            *pair(Y, Z, X, 2), *pair(Z, X, Y, 2),
-            *pair(Z, X, 2), *pair(X, Z, 2),
-            pltpu.VMEM((GX, GY, 2, width), jnp.float32),
-            dma(4),
-            dma(Y, Z, 2), dma(Y, Z, 2),
-            dma(Y, Z, X, 2), dma(Z, X, Y, 2),
-            dma(Z, X, 2), dma(X, Z, 2),
-            dma(regions), dma(GX, GY),
+            *pair(Y - 1, Z, X, 2), *pair(Z, X, Y, 2),
+            *pair(Z * X - 1, 2), *pair(X, Z, 2),
+            pltpu.VMEM((regions, 2, width), jnp.float32),
+            dma(4), dma(7),
+            dma(Y, Z), dma(Y - 1, Z, X), dma(X, Z), pltpu.SemaphoreType.DMA,
             pltpu.SemaphoreType.REGULAR, pltpu.SemaphoreType.REGULAR,
         ],
         compiler_params=pltpu.CompilerParams(collective_id=0, has_side_effects=True),

time: 26.1 us -> 24.4 us (0.935)
  Pallas kernels: 25.3 us -> 23.6 us
    pallas_call x1, Pallas kernels: 24.6 us -> 22.9 us  [shards(): pl.pallas_call(functools.partial(kernel, (GX, GY, X, Y, Z)), out_shape=(p...]
where the time goes in v2:
time: 24.4 us; the launch traced here: 24.3 us
  Pallas kernels  23.6 us (97%)
  between operations  0.64 us (3%)
    pallas_call x1, Pallas kernels, shards(): pl.pallas_call(functools.partial(kernel, (GX, GY, X, Y, Z)), out_shape=(p...  22.9 us
    pallas_call x1, Pallas kernels, shards(): pl.pallas_call(finish, out_shape=(jax.ShapeDtypeStruct((2, band, width),...  0.71 us

profile of v2, /device:TPU:0, one launch (start us, length us, event | category | flops | bytes accessed | tf_op | source)
XLA Modules:
  0.0 24.3 jit_solution(17225946133399589818)
XLA Ops:
  0.6 22.9 %shard_map.67 = (s32[2,16,128]{2,1,0:T(8,128)S(1)}, bf16[2,3,16,128]{3,2,1,0:T(8,128)(2,1)S(1)}, f32[32,2,128]{2,1,0:T(2,128)S(1)}) custom-call(s32[32]{0:T(128)} %own_hbm.1, s32[1,32]{1,0:T(1,128)} %slots_hbm.1, s32[32,16,128]{2,1,0:T(8,128)} %bitcast.10, bf16[32,3,16,128]{3,2,1,0:T(8,128)(2,1)} %bitcast.9), custom_call_target="tpu_custom_call" | custom-call | tf_op jit(solution)/shard_map/pallas_call | solution.py:350
  23.6 0.7 %shard_map.68 = (s32[2,16,128]{2,1,0:T(8,128)}, bf16[2,3,16,128]{3,2,1,0:T(8,128)(2,1)}, f32[3,32,64]{2,1,0:T(8,128)}) custom-call(s32[2,16,128]{2,1,0:T(8,128)S(1)} %get-tuple-element.9.in_d, bf16[2,3,16,128]{3,2,1,0:T(8,128)(2,1)S(1)} %get-tuple-element.10.in_c, f32[32,2,128]{2,1,0:T(2,128)S(1)} %get-tuple-element.11.in_t), custom_call_target="tpu_custom_call" | custom-call | tf_op jit(solution)/shard_map/pallas_call | solution.py:374

commit v3 on v2

--- a/solution.py
+++ b/solution.py
@@ -9,6 +9,8 @@
 
 FAR = 1073741824
 HALF = 536870912
+LOWEST = -2147483648
+LARGEST = 2147483647
 MESH = pl.DeviceIdType.MESH
 
 
@@ -24,6 +26,19 @@
     nearer = key_b < key_a
     key = jnp.minimum(key_a, key_b)
     return key, [jnp.where(nearer, b, a) for a, b in zip(colors_a, colors_b)]
+
+
+def merge_tagged(first, second):
+    key, colors = merge(first, second)
+    unnamed = first[1][0] < 0
+    return key, [jnp.where(unnamed, b, c) for b, c in zip(second[1], colors)]
+
+
+def fold(values, how):
+    total = values[0]
+    for value in values[1:]:
+        total = how(total, value)
+    return total
 
 
 def load(ref_d, ref_c, index):
@@ -46,13 +61,37 @@
     return lax.rem(z + 1 + k, Z)
 
 
+def plan(X, Y, Z):
+    halves_a, halves_b = ((0,), (1,)) if X == 2 else ((0, 1), ())
+    first, second = [], []
+    for near in (False, True):
+        for k in range(Z):
+            for i in range(Y - 1):
+                for j in [X - 1] if near else range(X - 1):
+                    first += [("a", h, j, i, k) for h in halves_a]
+            for j in range(X - 1):
+                for i in [Y - 1] if near else range(Y - 1):
+                    first += [("b", h, j, i, k) for h in halves_b]
+    for k in range(Z):
+        second += [("a", h, j, Y - 1, k) for j in range(X) for h in halves_a]
+        second += [("b", h, X - 1, i, k) for i in range(Y) for h in halves_b]
+    return halves_a, halves_b, first, second
+
+
+def sent_tiles(X, Y, Z):
+    halves_a, halves_b, first, second = plan(X, Y, Z)
+    na, nb = len(halves_a), len(halves_b)
+    rest = na * (X * (Z - 1) + X - 1) + nb * (Z * (Y - 1) + Z - 1)
+    return len(first) * 2 + len(second) + rest
+
+
 def kernel(
     dims, own_hbm, slots_hbm, depth_hbm, color_hbm,
     out_d, out_c, out_t,
     own_ref, slots_ref, tab_ref, depth_ref, color_ref,
-    cs_d, cs_c, cr_d, cr_c, ys_d, ys_c, yr_d, yr_c, zs_d, zs_c, zr_d, zr_c,
+    s_d, s_c, cr_d, cr_c, ay_d, ay_c, az_d, az_c, ax_d, ax_c, bx_d, bx_c, by_d, by_c, bz_d, bz_c,
     gath,
-    l_sem, s_sem, c_rs, y_rs, z_rs, g_rs, tok_lo, tok_hi,
+    l_sem, s_sem, c_rs, ay_rs, az_rs, ax_rs, bx_rs, by_rs, bz_rs, g_rs, tok_lo, tok_hi,
 ):
     GX, GY, X, Y, Z = dims
     regions = GX * GY
@@ -102,7 +141,7 @@
         local(color_hbm, color_ref.at[pl.ds(0, slots)], 3),
     ]
 
-    def token(which):
+    def token():
         @pl.when(has_lo)
         def _():
             pl.semaphore_signal(tok_hi, inc=1, device_id=at(core, x, y, z - 1), device_id_type=MESH)
@@ -122,7 +161,7 @@
 
     depth_ref[slots] = jnp.full(depth_ref.shape[1:], FAR, jnp.int32)
     for c in range(3):
-        color_ref[slots, c] = jnp.zeros(color_ref.shape[2:], jnp.bfloat16)
+        color_ref[slots, c] = jnp.full(color_ref.shape[2:], -1.0, jnp.bfloat16)
 
     loads[0].wait()
     loads[1].wait()
@@ -163,98 +202,161 @@
             live = (row >= top) & (row <= bottom) & in_col
             tab_ref[p * 2 + h] = jnp.where(live, (row - top) * width + (col - left), slots)
 
-    def own_tile(cc, xx, yy, zz, h):
+    def own_tile(kind, cc, xx, yy, zz, h):
         slot = tab_ref[((xx * 2 + cc) * GY + zz * Y + yy) * 2 + h]
-        return (depth_ref[slot] - HALF) * 2 + core, [color_ref[slot, c] for c in range(3)]
+        depth = depth_ref[slot] - HALF
+        if kind == "a":
+            key = depth * 2 + core
+        else:
+            key = jnp.maximum(depth * 4 + (x * 2 + core), jnp.where(slot == slots, LARGEST, LOWEST))
+        return key, [color_ref[slot, c] for c in range(3)]
 
     def remote(src, dst, ss, rs, device):
         return pltpu.make_async_remote_copy(
             src_ref=src, dst_ref=dst, send_sem=ss, recv_sem=rs, device_id=device, device_id_type=MESH
         )
 
-    def send(pairs, which, rs, device):
-        for k, (src, dst) in enumerate(pairs):
-            remote(src, dst, s_sem.at[which + k], rs, device).start()
+    used = [0]
+
+    def post(value):
+        n = used[0]
+        used[0] += 1
+        store(s_d, s_c, (n,), value)
+        return n
+
+    def send(n, many, into_d, into_c, at_index, rs, device):
+        if many is None:
+            src, dst = (n,), (at_index,)
+        else:
+            src, dst = (pl.ds(n, many),), (pl.ds(at_index, many),)
+        remote(s_d.at[src], into_d.at[dst], s_sem.at[0], rs, device).start()
+        remote(s_c.at[src], into_c.at[dst], s_sem.at[1], rs, device).start()
 
     def take(ref, rs):
         remote(ref, ref, s_sem.at[0], rs, (gx, gy)).wait_recv()
 
-    def arrived(units, rs):
-        take(depth_ref.at[pl.ds(0, 5 * units)], rs)
+    def arrived(tiles, rs):
+        if tiles % 2:
+            take(depth_ref.at[pl.ds(0, 5 * tiles), pl.ds(0, depth_ref.shape[1] // 2)], rs)
+        else:
+            take(depth_ref.at[pl.ds(0, 5 * tiles // 2)], rs)
 
     def drained(ref, which):
         remote(ref, ref, s_sem.at[which], g_rs, (gx, gy)).wait_send()
 
-    targets_y = [lax.rem(y + 1 + i, Y) for i in range(Y)]
-    targets_z = [far_pos(z, k, Z) for k in range(Z)]
-    targets_x = [lax.rem(x + 1 + j, X) for j in range(X)]
+    ty = [lax.rem(y + 1 + i, Y) for i in range(Y)]
+    tz = [far_pos(z, k, Z) for k in range(Z)]
+    tx = [lax.rem(x + 1 + j, X) for j in range(X)]
+    halves_a, halves_b, first, second = plan(X, Y, Z)
+    na, nb = len(halves_a), len(halves_b)
+    tiles = first + second
+    chunk = len(tiles) // c_rs.shape[0]
 
     loads[2].wait()
     loads[3].wait()
 
-    for i in range(Y):
-        for k in range(Z):
-            for j in range(X):
-                for h in range(2):
-                    store(cs_d, cs_c, (i, k, j, h), own_tile(1 - core, targets_x[j], targets_y[i], targets_z[k], h))
-            if i == 0 and k == 0:
-                near = X + Y - 1 + jnp.where(has_lo, 1, 0) + jnp.where(has_hi, 1, 0)
-                pl.semaphore_wait(barrier, near)
-            send(
-                [(cs_d.at[i, k], cr_d.at[i, k]), (cs_c.at[i, k], cr_c.at[i, k])],
-                0, c_rs.at[i, k],
-                at(1 - core, x, y, z),
-            )
-        if i == 0:
-            token(0)
-
-    for i in range(Y):
-        mine = i == Y - 1
-        for k in range(Z):
-            arrived(X, c_rs.at[i, k])
-            for j in range(X):
-                for h in range(2):
-                    value = merge(
-                        own_tile(core, targets_x[j], targets_y[i], targets_z[k], h),
-                        load(cr_d, cr_c, (i, k, j, h)),
-                    )
-                    if mine:
-                        store(yr_d, yr_c, (k, j, y, h), value)
-                    else:
-                        store(ys_d, ys_c, (i, k, j, h), value)
-                if not mine:
-                    send(
-                        [(ys_d.at[i, k, j], yr_d.at[k, j, y]), (ys_c.at[i, k, j], yr_c.at[k, j, y])],
-                        2, y_rs.at[i, k, j],
-                        at(core, x, targets_y[i], z),
-                    )
-        if i == 0:
-            take_token()
-            token(1)
-
+    for q in range(c_rs.shape[0]):
+        for kind, h, j, i, k in tiles[q * chunk : (q + 1) * chunk]:
+            n = post(own_tile(kind, 1 - core, tx[j], ty[i], tz[k], h))
+        if q == 0:
+            near = X + Y - 1 + jnp.where(has_lo, 1, 0) + jnp.where(has_hi, 1, 0)
+            pl.semaphore_wait(barrier, near)
+        send(q * chunk, chunk, cr_d, cr_c, q * chunk, c_rs.at[q], at(1 - core, x, y, z))
+        if q == 0:
+            token()
+
+    def ay_at(h, j, k, yy):
+        return ((k * X + j) * na + halves_a.index(h)) * Y + yy
+
+    def az_at(h, j, zz):
+        return (j * na + halves_a.index(h)) * Z + zz
+
+    def ax_at(h, xx):
+        return halves_a.index(h) * X + xx
+
+    def bx_at(h, i, k, xx):
+        return ((k * Y + i) * nb + halves_b.index(h)) * X + xx
+
+    def by_at(h, k, yy):
+        return (k * nb + halves_b.index(h)) * Y + yy
+
+    def bz_at(h, zz):
+        return halves_b.index(h) * Z + zz
+
+    for n, (kind, h, j, i, k) in enumerate(tiles):
+        if n % chunk == 0:
+            arrived(chunk, c_rs.at[n // chunk])
+        how = merge if kind == "a" else merge_tagged
+        value = how(own_tile(kind, core, tx[j], ty[i], tz[k], h), load(cr_d, cr_c, (n,)))
+        if n >= len(first):
+            if kind == "a":
+                store(ay_d, ay_c, (ay_at(h, j, k, y),), value)
+            else:
+                store(bx_d, bx_c, (bx_at(h, i, k, x),), value)
+        elif kind == "a":
+            send(post(value), None, ay_d, ay_c, ay_at(h, j, k, y), ay_rs.at[i, k, j, halves_a.index(h)], at(core, x, ty[i], z))
+        else:
+            send(post(value), None, bx_d, bx_c, bx_at(h, i, k, x), bx_rs.at[j, k, i, halves_b.index(h)], at(core, tx[j], y, z))
+        if n == len(first) - 1:
+            for _ in range(Z - 3):
+                take_token()
+                token()
     take_token()
-    token(2)
-    take_token()
+
+    def step_a(j, k):
+        for h in halves_a:
+            for i in range(Y - 1):
+                arrived(1, ay_rs.at[i, k, j, halves_a.index(h)])
+            value = fold([load(ay_d, ay_c, (ay_at(h, j, k, q),)) for q in range(Y)], merge)
+            if k == Z - 1:
+                store(az_d, az_c, (az_at(h, j, z),), value)
+            else:
+                send(post(value), None, az_d, az_c, az_at(h, j, z), az_rs.at[k, j, halves_a.index(h)], at(core, x, y, tz[k]))
+
+    def step_bx(i, k):
+        for h in halves_b:
+            for j in range(X - 1):
+                arrived(1, bx_rs.at[j, k, i, halves_b.index(h)])
+            value = fold([load(bx_d, bx_c, (bx_at(h, i, k, q),)) for q in range(X)], merge_tagged)
+            if i == Y - 1:
+                store(by_d, by_c, (by_at(h, k, y),), value)
+            else:
+                send(post(value), None, by_d, by_c, by_at(h, k, y), by_rs.at[i, k, halves_b.index(h)], at(core, x, ty[i], z))
+
+    def step_by(k):
+        for h in halves_b:
+            for i in range(Y - 1):
+                arrived(1, by_rs.at[i, k, halves_b.index(h)])
+            value = fold([load(by_d, by_c, (by_at(h, k, q),)) for q in range(Y)], merge_tagged)
+            if k == Z - 1:
+                store(bz_d, bz_c, (bz_at(h, z),), value)
+            else:
+                send(post(value), None, bz_d, bz_c, bz_at(h, z), bz_rs.at[k, halves_b.index(h)], at(core, x, y, tz[k]))
 
     for k in range(Z):
-        for j in range(X):
-            for i in range(Y - 1):
-                arrived(1, y_rs.at[i, k, j])
-            mine = k == Z - 1 and j == X - 1
-            for h in range(2):
-                value = load(yr_d, yr_c, (k, j, 0, h))
-                for q in range(1, Y):
-                    value = merge(value, load(yr_d, yr_c, (k, j, q, h)))
-                if mine:
-                    store(zr_d, zr_c, (x, z, h), value)
-                else:
-                    store(zs_d, zs_c, (k * X + j, h), value)
-            if not mine:
-                send(
-                    [(zs_d.at[k * X + j], zr_d.at[x, z]), (zs_c.at[k * X + j], zr_c.at[x, z])],
-                    4, z_rs.at[x, z],
-                    at(core, targets_x[j], y, targets_z[k]),
-                )
+        for i in range(Y - 1):
+            step_bx(i, k)
+        for j in range(X - 1):
+            step_a(j, k)
+    for k in range(Z):
+        step_a(X - 1, k)
+        step_bx(Y - 1, k)
+    for k in range(Z):
+        step_by(k)
+
+    def step_az(j):
+        for h in halves_a:
+            for k in range(Z - 1):
+                arrived(1, az_rs.at[k, j, halves_a.index(h)])
+            key, colors = fold([load(az_d, az_c, (az_at(h, j, q),)) for q in range(Z)], merge)
+            value = (key >> 1, colors)
+            if j == X - 1:
+                store(ax_d, ax_c, (ax_at(h, x),), value)
+            else:
+                send(post(value), None, ax_d, ax_c, ax_at(h, x), ax_rs.at[j, halves_a.index(h)], at(core, tx[j], y, z))
+
+    for j in range(X):
+        step_az(j)
 
     lane_k = lax.broadcasted_iota(jnp.int32, (128, 128), 0) // 8
     lane_l = lax.broadcasted_iota(jnp.int32, (128, 128), 1)
@@ -263,28 +365,24 @@
         hit = (lane_l == lane_k + 32 * h) | (lane_l == lane_k + 32 * h + 80)
         groups.append(jnp.where(hit, 1.0 / 64.0, 0.0).astype(jnp.bfloat16))
 
-    for k in range(Z):
-        for j in range(X):
-            if k == Z - 1 and j == X - 1:
-                continue
-            xx, zz = targets_x[j], targets_z[k]
-            arrived(1, z_rs.at[xx, zz])
-
     sums = [None] * 3
     row = lax.broadcasted_iota(jnp.int32, (16, 128), 0)
     lane = lax.broadcasted_iota(jnp.int32, (16, 128), 1)
     keep = (row < 8) == (lane < 64)
-    for h in range(2):
-        value = None
-        for xx in range(X):
-            part = load(zr_d, zr_c, (xx, 0, h))
-            for zz in range(1, Z):
-                part = merge(part, load(zr_d, zr_c, (xx, zz, h)))
-            part = (part[0] >> 1, part[1])
-            value = part if value is None else merge(value, part)
-        out_d[h] = value[0] + HALF
+    for h in halves_b + halves_a:
+        if h in halves_b:
+            for k in range(Z - 1):
+                arrived(1, bz_rs.at[k, halves_b.index(h)])
+            key, colors = fold([load(bz_d, bz_c, (bz_at(h, q),)) for q in range(Z)], merge_tagged)
+            depth = jnp.where(colors[0].astype(jnp.float32) < 0, FAR, (key >> 2) + HALF)
+        else:
+            for j in range(X - 1):
+                arrived(1, ax_rs.at[j, halves_a.index(h)])
+            key, colors = fold([load(ax_d, ax_c, (ax_at(h, q),)) for q in range(X)], merge)
+            depth = key + HALF
+        out_d[h] = depth
         for c in range(3):
-            color = value[1][c]
+            color = jnp.maximum(colors[c], jnp.zeros((), jnp.bfloat16))
             out_c[h, c] = color
             part = jnp.dot(color, groups[h], preferred_element_type=jnp.float32)
             part = jnp.where(keep, part, 0.0)
@@ -302,20 +400,16 @@
         for j in range(X):
             for i in range(Y):
                 for cc in (1 - core, core):
-                    others.append(at(cc, targets_x[j], targets_y[i], targets_z[k]))
+                    others.append(at(cc, tx[j], ty[i], tz[k]))
     others.pop()
     for device in others:
-        remote(gath.at[rank], gath.at[rank], s_sem.at[6], g_rs, device).start()
+        remote(gath.at[rank], gath.at[rank], s_sem.at[2], g_rs, device).start()
     take(gath.at[pl.ds(0, regions - 1)], g_rs)
     for r in range(regions):
         out_t[r] = gath[own_ref[r]]
-    drained(cs_d, 0)
-    drained(cs_c, 1)
-    drained(ys_d, 2)
-    drained(ys_c, 3)
-    drained(zs_d, 4)
-    drained(zs_c, 5)
-    drained(gath.at[pl.ds(0, regions - 1)], 6)
+    drained(s_d, 0)
+    drained(s_c, 1)
+    drained(gath.at[pl.ds(0, regions - 1)], 2)
 
 
 def finish(in_d, in_c, in_t, out_d, out_c, out_t):
@@ -334,6 +428,7 @@
     X, Z = GX // 2, 4
     Y = GY // Z
     regions = GX * GY
+    na, nb = (len(halves) for halves in plan(X, Y, Z)[:2])
     slots, band, width = slot_depth.shape[1:]
     depth = slot_depth[0]
     color = jnp.transpose(slot_color[0], (0, 2, 1, 3))
@@ -361,12 +456,14 @@
             pltpu.SMEM((1, slots), jnp.int32),
             pltpu.SMEM((2 * regions,), jnp.int32),
             *pair(slots + 1),
-            *pair(Y, Z, X, 2), *pair(Y, Z, X, 2),
-            *pair(Y - 1, Z, X, 2), *pair(Z, X, Y, 2),
-            *pair(Z * X - 1, 2), *pair(X, Z, 2),
+            *pair(sent_tiles(X, Y, Z)), *pair(regions),
+            *pair(na * X * Z * Y), *pair(na * X * Z), *pair(na * X),
+            *pair(max(nb * X * Z * Y, 1)), *pair(max(nb * Z * Y, 1)), *pair(max(nb * Z, 1)),
             pltpu.VMEM((regions, 2, width), jnp.float32),
-            dma(4), dma(7),
-            dma(Y, Z), dma(Y - 1, Z, X), dma(X, Z), pltpu.SemaphoreType.DMA,
+            dma(4), dma(3), dma(8),
+            dma(Y - 1, Z, X, na), dma(Z - 1, X, na), dma(X - 1, na),
+            dma(X - 1, Z, Y, max(nb, 1)), dma(Y - 1, Z, max(nb, 1)), dma(Z - 1, max(nb, 1)),
+            pltpu.SemaphoreType.DMA,
             pltpu.SemaphoreType.REGULAR, pltpu.SemaphoreType.REGULAR,
         ],
         compiler_params=pltpu.CompilerParams(collective_id=0, has_side_effects=True),

time: 24.4 us -> 22.6 us (0.926)
  Pallas kernels: 23.6 us -> 21.8 us
    pallas_call x1, Pallas kernels: 22.9 us -> 21.1 us  [shards(): pl.pallas_call(functools.partial(kernel, (GX, GY, X, Y, Z)), out_shape=(p...]
where the time goes in v3:
time: 22.6 us; the launch traced here: 22.4 us
  Pallas kernels  21.8 us (96%)
  between operations  0.64 us (3%)
    pallas_call x1, Pallas kernels, shards(): pl.pallas_call(functools.partial(kernel, (GX, GY, X, Y, Z)), out_shape=(p...  21.1 us
    pallas_call x1, Pallas kernels, shards(): pl.pallas_call(finish, out_shape=(jax.ShapeDtypeStruct((2, band, width),...  0.71 us

profile of v3, /device:TPU:0, one launch (start us, length us, event | category | flops | bytes accessed | tf_op | source)
XLA Modules:
  0.0 22.4 jit_solution(12868127912442348029)
XLA Ops:
  0.6 21.1 %shard_map.67 = (s32[2,16,128]{2,1,0:T(8,128)S(1)}, bf16[2,3,16,128]{3,2,1,0:T(8,128)(2,1)S(1)}, f32[32,2,128]{2,1,0:T(2,128)S(1)}) custom-call(s32[32]{0:T(128)} %own_hbm.1, s32[1,32]{1,0:T(1,128)} %slots_hbm.1, s32[32,16,128]{2,1,0:T(8,128)} %bitcast.10, bf16[32,3,16,128]{3,2,1,0:T(8,128)(2,1)} %bitcast.9), custom_call_target="tpu_custom_call" | custom-call | tf_op jit(solution)/shard_map/pallas_call | solution.py:445
  21.7 0.7 %shard_map.68 = (s32[2,16,128]{2,1,0:T(8,128)}, bf16[2,3,16,128]{3,2,1,0:T(8,128)(2,1)}, f32[3,32,64]{2,1,0:T(8,128)}) custom-call(s32[2,16,128]{2,1,0:T(8,128)S(1)} %get-tuple-element.9.in_d, bf16[2,3,16,128]{3,2,1,0:T(8,128)(2,1)S(1)} %get-tuple-element.10.in_c, f32[32,2,128]{2,1,0:T(2,128)S(1)} %get-tuple-element.11.in_t), custom_call_target="tpu_custom_call" | custom-call | tf_op jit(solution)/shard_map/pallas_call | solution.py:471
